TPU v7x, 32 devices: a whole 2x2x4 slice. The times are simulated.
32 devices in a mesh: tm: 8 (over y, x, core), cell: 4 (over z).
Axes of the slice: x: 2, y: 2, z: 4, core: 2. Of those that a mesh axis runs over, the one named last changes fastest.
Arguments:
- anomalies: bfloat16 [24, 2, 8192, 256], P('tm', None, 'cell'), may hold values from -6 to 6
- obs_cells: int32 [24, 128], P('tm', 'cell'), may hold values from 0 to 8191, as said below
- obs_counts: int32 [24, 4], P('tm', 'cell'), may hold values from 16 to 32
- obs_precision: float32 [24, 128], P('tm', 'cell'), may hold values from 0.1 to 1
- inflation: float32 [24], P('tm'), may hold values from 1 to 1.12
Outputs:
- smoothed: bfloat16 [24, 2, 8192, 256], P('tm', None, 'cell')
Inputs may be any that keep to these rules, and one draw needn't show every extreme that they name: `obs_cells`: slot k of a window names a cell of the block of 2048 cells that starts at (k // 32) * 2048; two slots may name the same cell.
All inputs are finite; a program needn't handle non-finite values.
Results may differ from a plain program's by a relative error of at most 0.017.
Values may be sent and summed in bfloat16 or wider, within the bound.
A program may use at most 128 MiB of HBM per device.

v0:
```python
import jax
import jax.numpy as jnp
from jax import lax
from jax.sharding import PartitionSpec as P


def matmul_f32(left, right):
    return jnp.dot(left, right, precision=lax.Precision.HIGHEST, preferred_element_type=jnp.float32)


def gram_of(picked, weights):
    as_float = picked.astype(jnp.float32)
    weighted = as_float * weights[:, :, None]
    return jnp.einsum(
        "wkm,wkn->wmn",
        weighted,
        as_float,
        precision=lax.Precision.HIGHEST,
        preferred_element_type=jnp.float32,
    )


def transform_of(gram, rho):
    members = gram.shape[-1]
    unit_matrix = jnp.eye(members, dtype=jnp.float32)
    factor = jnp.linalg.cholesky((members - 1.0) * unit_matrix[None] + gram)
    inverse = jax.vmap(
        lambda lower_f: jax.scipy.linalg.solve_triangular(lower_f, unit_matrix, lower=True)
    )(factor)
    scale = rho * jnp.sqrt(jnp.float32(members - 1.0))
    return scale[:, None, None] * jnp.swapaxes(inverse, 1, 2)


def local(anomalies, obs_cells, obs_counts, obs_precision, inflation):
    cell_width = anomalies.shape[2]
    members = anomalies.shape[3]
    slots = obs_cells.shape[1]
    first_cell = lax.axis_index("cell") * cell_width
    offsets = obs_cells - first_cell
    picked = jax.vmap(lambda field, where_at: field[0][where_at])(anomalies, offsets)
    live = jnp.arange(slots, dtype=jnp.int32)[None, :] < obs_counts
    picked = jnp.where(live[:, :, None], picked, jnp.zeros_like(picked))
    weights = jnp.where(live, obs_precision, jnp.float32(0.0))
    gathered, gathered_weights = (
        lax.all_gather(picked, "cell", axis=1, tiled=True),
        lax.all_gather(weights.astype(jnp.bfloat16), "cell", axis=1, tiled=True).astype(
            weights.dtype
        ),
    )
    gram = gram_of(gathered, gathered_weights)
    transforms = transform_of(gram, inflation)
    windows = transforms.shape[0]
    partial_list = [transforms[windows - 1]]
    for window in range(windows - 2, -1, -1):
        partial_list.insert(0, matmul_f32(transforms[window], partial_list[0]))
    own_product = partial_list[0]
    unit_matrix = jnp.eye(members, dtype=jnp.float32)
    products = lax.all_gather(
        own_product[None].astype(jnp.bfloat16), "tm", axis=0, tiled=True
    ).astype(jnp.float32)
    count = lax.axis_size("tm")
    position = lax.axis_index("tm")

    def absorb(turn, carried):
        source = count - 1 - turn
        updated = matmul_f32(products[source], carried)
        return jnp.where(source > position, updated, carried)

    later_product = lax.fori_loop(0, count, absorb, unit_matrix)
    suffixes = jnp.stack(
        [matmul_f32(partial_value, later_product) for partial_value in partial_list]
    )
    weight_mats = suffixes.astype(jnp.bfloat16)
    flat = anomalies.reshape(windows, 2 * cell_width, members)
    result = jnp.einsum("wcm,wmn->wcn", flat, weight_mats, preferred_element_type=jnp.float32)
    return result.astype(jnp.bfloat16).reshape(anomalies.shape)


def solution(mesh):
    placed = (
        P("tm", None, "cell", None),
        P("tm", "cell"),
        P("tm", "cell"),
        P("tm", "cell"),
        P("tm"),
    )
    return jax.shard_map(
        local, mesh=mesh, in_specs=placed, out_specs=P("tm", None, "cell", None), check_vma=False
    )
```

profile of v0, /device:TPU:0, one launch (start us, length us, event | category | flops | bytes accessed | tf_op | source)
XLA Modules:
  0.0 269.0 jit_solution(16111272196419085937)
XLA Ops:
  6.5 0.0 all-gather.4.cloned.1.call-start
  6.5 0.5 iota_multiply_fusion
  7.0 0.6 iota_compare_fusion.4
  7.7 0.6 iota_compare_fusion.3
  8.3 0.6 iota_compare_fusion.2
  8.9 0.8 fusion.21
  9.8 0.7 iota_compare_fusion.5
  10.5 0.7 broadcast_multiply_fusion
  11.2 0.8 fusion.35
  11.9 0.7 fusion.34
  12.6 0.1 reshape.87
  12.7 12.6 %all-gather.1 = bf16[4,32,3]{1,2,0:T(4,128)(2,1)S(1)} all-gather(bf16[1,32,3]{1,2,0:T(4,128)(2,1)S(1)} %fusion.35), channel_id=1, replica_groups=mesh['tm'=8,'cell'=4] {'cell'}, dimensions={0}, use_global_device_ids=true | all-gather | bytes 960 | tf_op jit(solution)/shard_map/all_gather | solution.py:46
  25.3 0.1 reshape.102
  25.4 0.7 fusion.38
  26.1 2.1 slice_bitcast_fusion
  28.2 2.2 gather_fusion
  30.4 0.9 broadcast_select_fusion
  31.3 13.6 %all_gather.9 = bf16[3,128,256]{2,1,0:T(8,128)(2,1)S(1)} all-gather(bf16[3,32,256]{2,1,0:T(8,128)(2,1)S(1)} %broadcast_select_fusion), channel_id=1, replica_groups=mesh['tm'=8,'cell'=4] {'cell'}, dimensions={1}, use_global_device_ids=true | all-gather | bytes 245760 | tf_op jit(solution)/shard_map/all_gather | solution.py:45
  44.9 0.6 fusion.15
  45.5 0.0 copy-start
  45.5 0.3 copy.52
  45.7 1.2 fusion.9
  46.9 35.2 %custom-call.17 = f32[3,128,128]{2,1,0:T(8,128)S(1)} custom-call(f32[3,128,128]{2,1,0:T(8,128)S(1)} %cholesky.122), custom_call_target="Cholesky" | custom-call | tf_op jit(solution)/shard_map/jit(cholesky)/cholesky | solution.py:26
  82.1 0.0 copy-done.3
  82.1 29.5 %custom-call.18 = f32[3,1,128,128]{2,3,1,0:T(8,128)S(1)} custom-call(f32[3,1,128,128]{3,2,1,0:T(8,128)S(1)} %select_bitcast_fusion), custom_call_target="InvertDiagBlocksLowerTriangular" | custom-call | tf_op jit(solution)/shard_map/jit(cholesky)/cholesky | solution.py:26
  111.6 0.1 cholesky.117
  111.7 0.4 constant_dynamic-update-slice_fusion.1
  112.1 0.5 convolution_subtract_fusion.1
  112.6 35.2 %custom-call.19 = f32[3,128,128]{2,1,0:T(8,128)S(1)} custom-call(f32[3,128,128]{2,1,0:T(8,128)S(1)} %convolution_subtract_fusion.1), custom_call_target="Cholesky" | custom-call | tf_op jit(solution)/shard_map/jit(cholesky)/cholesky | solution.py:26
  147.8 0.0 copy-done.2
  147.8 0.1 compare_reduce_fusion
  148.0 0.1 compare_reduce_fusion.1
  148.1 0.0 copy-done.1
  148.1 0.2 select_select_fusion
  148.3 0.1 triangular_solve.74
  148.3 5.4 %while.17 = (s32[]{:T(128)}, f32[3,256,256]{2,1,0:T(8,128)S(1)}, s32[2,2]{1,0:T(2,128)S(1)}, f32[2,3,128,128]{3,2,0,1:T(8,128)}, s32[]{:T(128)}) while((s32[]{:T(128)}, f32[3,256,256]{2,1,0:T(8,128)S(1)}, s32[2,2]{1,0:T(2,128)S(1)}, f32[2,3,128,128]{3,2,0,1:T(8,128)}, s32[]{:T(128)}) %tuple.56), condition=%wide.while_cond, body=%wide.while_body.sunk | while | flops 2 | bytes 394349 | solution.py:28
  148.3 0.6 fusion.58
  148.9 2.1 bitcast_dynamic-update-slice_fusion.2
  151.0 0.6 fusion.58
  151.6 2.1 bitcast_dynamic-update-slice_fusion.2
  153.7 59.8 %custom-call.20 = f32[3,2,128,128]{2,3,1,0:T(8,128)S(1)} custom-call(f32[3,2,128,128]{3,2,1,0:T(8,128)} %bitcast.105), custom_call_target="InvertDiagBlocksLowerTriangular" | custom-call | tf_op jit(solution)/shard_map/vmap(jit(_solve_triangular))/triangular_solve | solution.py:28
  213.5 0.5 fusion.25
  214.1 0.5 convolution_subtract_fusion
  214.5 0.5 fusion.24
  215.1 0.1 fusion.7
  215.2 0.6 fusion.18
  215.8 1.3 fusion.39
  217.1 0.0 all-gather.4.cloned.1.call-update
  217.2 21.8 %all-gather.4.cloned.1.call-done = bf16[2048,256]{1,0:T(8,128)(2,1)} async-done(((bf16[256,256]{1,0:T(8,128)(2,1)}), bf16[2048,256]{1,0:T(8,128)(2,1)}) %all-gather.4.cloned.1.call-update) | async-done | bytes 1048592 | tf_op jit(solution)/shard_map/all_gather | solution.py:58
  238.9 1.4 convert.15
  240.4 3.5 %while.16 = (s32[]{:T(128)}, f32[256,256]{1,0:T(8,128)S(1)}, s32[]{:T(128)}, f32[8,256,256]{2,1,0:T(8,128)S(1)}, s32[]{:T(128)}, /*index=5*/s32[]{:T(128)}, s32[]{:T(128)}, s32[]{:T(128)}) while((s32[]{:T(128)}, f32[256,256]{1,0:T(8,128)S(1)}, s32[]{:T(128)}, f32[8,256,256]{2,1,0:T(8,128)S(1)}, s32[]{:T(128)}, /*index=5*/s32[]{:T(128)}, ...), condition=%wide.region_5.6_spmd, body=%wide.region_4.5_spmd.sunk | while | flops 201392128 | bytes 1573017 | solution.py:69
  240.4 0.4 convolution_select_fusion.2
  240.9 0.4 convolution_select_fusion.2
  241.3 0.4 convolution_select_fusion.2
  241.7 0.4 convolution_select_fusion.2
  242.2 0.4 convolution_select_fusion.2
  242.6 0.4 convolution_select_fusion.2
  243.1 0.4 convolution_select_fusion.2
  243.5 0.4 convolution_select_fusion.2
  243.9 0.6 fusion.6
  244.5 0.4 fusion.5
  244.9 1.3 fusion.4
  246.2 7.3 %fusion.3 = bf16[3,4096,256]{1,2,0:T(8,128)(2,1)} fusion(bf16[3,4096,256]{2,1,0:T(8,128)(2,1)} %bitcast.99, bf16[1,256,256]{2,1,0:T(8,128)(2,1)S(1)} %fusion.6, bf16[1,256,256]{2,1,0:T(8,128)(2,1)S(1)} %fusion.5, bf16[1,256,256]{2,1,0:T(8,128)(2,1)S(1)} %fusion.4), kind=kOutput, calls=%fused_computation.8 | convolution fusion | flops 1614151680 | bytes 12976128 | tf_op jit(solution)/shard_map/wcm,wmn->wcn/dot_general | solution.py:75
  253.5 8.6 %copy.65 = bf16[3,4096,256]{2,1,0:T(8,128)(2,1)} copy(bf16[3,4096,256]{1,2,0:T(8,128)(2,1)} %fusion.3) | data formatting | bytes 12582912 | tf_op jit(solution)/shard_map/reshape | solution.py:76
  (23 shorter events, 0.3 us)
Async XLA Ops:
  6.5 232.4 %all-gather.4.cloned.1.call-start = ((), (), s32[]{:S(2)}) async-start(), calls=%async_computation | async-start | bytes 1179648 | tf_op jit(solution)/shard_map/all_gather | solution.py:58
  30.3 51.8 %copy-start.3 = (pred[128,128]{1,0:T(8,128)(4,1)S(1)}, pred[128,128]{1,0:T(8,128)(4,1)}, u32[]{:S(2)}) copy-start(pred[128,128]{1,0:T(8,128)(4,1)} %iota_compare_fusion.3) | copy-start | bytes 49156
  30.3 117.4 %copy-start.2 = (pred[128,128]{1,0:T(8,128)(4,1)S(1)}, pred[128,128]{1,0:T(8,128)(4,1)}, u32[]{:S(2)}) copy-start(pred[128,128]{1,0:T(8,128)(4,1)} %iota_compare_fusion.4) | copy-start | bytes 49156
  30.4 117.7 %copy-start.1 = (pred[256,256]{1,0:T(8,128)(4,1)S(1)}, pred[256,256]{1,0:T(8,128)(4,1)}, u32[]{:S(2)}) copy-start(pred[256,256]{1,0:T(8,128)(4,1)} %iota_compare_fusion.2) | copy-start | bytes 196612
  30.4 117.9 %copy-start.4 = (s32[2]{0:T(128)S(1)}, s32[2]{0:T(128)}, u32[]{:S(2)}) copy-start(s32[2]{0:T(128)} %iota_multiply_fusion) | copy-start | bytes 28
  45.5 168.1 %copy-start = (f32[128,256]{1,0:T(8,128)S(1)}, f32[128,256]{1,0:T(8,128)}, u32[]{:S(2)}) copy-start(f32[128,256]{1,0:T(8,128)} %get-tuple-element.145) | copy-start | bytes 393220
Sparse Core Ops, SparseCore 0:
  217.3 21.6 all-gather.3
where the time goes:
time: 270 us; the launch traced here: 269 us
  other arithmetic  170 us (63%)
  blocking collectives  26.2 us (10%)
  waiting for transfers between devices  21.8 us (8%)
  local copies, waits for them, and re-layouts  19.6 us (7%)
  matrix products  17.6 us (7%)
  between operations  13.6 us (5%)
    another operation x10, other arithmetic, transform_of(): factor = jnp.linalg.cholesky((members - 1.0) * unit_matrix[None] + gram)  101 us
    another operation x4, other arithmetic, transform_of(): jax.scipy.linalg.solve_triangular(lower_f, unit_matrix, lower=True)  61.1 us
    all_gather x1, waiting for transfers between devices, local(): lax.all_gather(own_product[None].astype(jnp.bfloat16), 'tm', axis=0, tile...  21.8 us
    all_gather x1, blocking collectives, local(): lax.all_gather(picked, 'cell', axis=1, tiled=True)  13.6 us
    all_gather x1, blocking collectives, local(): lax.all_gather(weights.astype(jnp.bfloat16), 'cell', axis=1, tiled=True)  12.6 us
    reshape x1, local copies, waits for them, and re-layouts, local(): return result.astype(jnp.bfloat16).reshape(anomalies.shape)  8.6 us
    dot_general x13, matrix products, matmul_f32(): jnp.dot(left, right, precision=lax.Precision.HIGHEST, preferred_element_t...  7.3 us
    dot_general x1, matrix products, local(): jnp.einsum('wcm,wmn->wcn', flat, weight_mats, preferred_element_type=jnp....  7.3 us
  transfers between devices with their start and end apart: 1, of which 1 were waited for; matrix products, arithmetic and copies ran while one was open for 0% of the time, Pallas kernels for 0%

commit v1 on v0

--- a/solution.py
+++ b/solution.py
@@ -2,6 +2,13 @@
 import jax.numpy as jnp
 from jax import lax
 from jax.sharding import PartitionSpec as P
+
+
+def gather_over(x, axis, d):
+    peers = lax.axis_size(axis)
+    blocks = jnp.stack([x for _ in range(peers)])
+    blocks = lax.all_to_all(blocks, axis, split_axis=0, concat_axis=0)
+    return jnp.concatenate(blocks, axis=d)
 
 
 def matmul_f32(left, right):
@@ -55,9 +62,7 @@
         partial_list.insert(0, matmul_f32(transforms[window], partial_list[0]))
     own_product = partial_list[0]
     unit_matrix = jnp.eye(members, dtype=jnp.float32)
-    products = lax.all_gather(
-        own_product[None].astype(jnp.bfloat16), "tm", axis=0, tiled=True
-    ).astype(jnp.float32)
+    products = gather_over(own_product[None].astype(jnp.bfloat16), "tm", 0).astype(jnp.float32)
     count = lax.axis_size("tm")
     position = lax.axis_index("tm")
 

time: 270 us -> 255 us (0.944)
  between operations: 13.6 us -> 0.25 us
  waiting for transfers between devices: 21.8 us -> 15.4 us
  starting transfers between devices: 0.01 us -> 4.24 us
    all_gather x1 -> x0, waiting for transfers between devices: 21.8 us -> none  [local(): lax.all_gather(own_product[None].astype(jnp.bfloat16), 'tm', axis=0, tile...]
    all_to_all x0 -> x1, waiting for transfers between devices: none -> 15.4 us  [gather_over(): blocks = lax.all_to_all(blocks, axis, split_axis=0, concat_axis=0)]
    all_to_all x0 -> x1, starting transfers between devices: none -> 4.24 us  [gather_over(): blocks = lax.all_to_all(blocks, axis, split_axis=0, concat_axis=0)]
    another operation x6 -> x7, local copies, waits for them, and re-layouts: 5.39 us -> 6.39 us
where the time goes in v1:
time: 255 us; the launch traced here: 254 us
  other arithmetic  170 us (67%)
  blocking collectives  26.2 us (10%)
  local copies, waits for them, and re-layouts  20.6 us (8%)
  matrix products  17.5 us (7%)
  waiting for transfers between devices  15.4 us (6%)
  starting transfers between devices  4.24 us (2%)
    another operation x10, other arithmetic, transform_of(): factor = jnp.linalg.cholesky((members - 1.0) * unit_matrix[None] + gram)  101 us
    another operation x4, other arithmetic, transform_of(): jax.scipy.linalg.solve_triangular(lower_f, unit_matrix, lower=True)  61.1 us
    all_to_all x1, waiting for transfers between devices, gather_over(): blocks = lax.all_to_all(blocks, axis, split_axis=0, concat_axis=0)  15.4 us
    all_gather x1, blocking collectives, local(): lax.all_gather(picked, 'cell', axis=1, tiled=True)  13.6 us
    all_gather x1, blocking collectives, local(): lax.all_gather(weights.astype(jnp.bfloat16), 'cell', axis=1, tiled=True)  12.6 us
    reshape x1, local copies, waits for them, and re-layouts, local(): return result.astype(jnp.bfloat16).reshape(anomalies.shape)  8.6 us
    dot_general x1, matrix products, local(): jnp.einsum('wcm,wmn->wcn', flat, weight_mats, preferred_element_type=jnp....  7.29 us
    dot_general x13, matrix products, matmul_f32(): jnp.dot(left, right, precision=lax.Precision.HIGHEST, preferred_element_t...  7.27 us
  transfers between devices with their start and end apart: 1, of which 1 were waited for; matrix products, arithmetic and copies ran while one was open for 0% of the time, Pallas kernels for 0%

profile of v1, /device:TPU:0, one launch (start us, length us, event | category | flops | bytes accessed | tf_op | source)
XLA Modules:
  0.0 254.4 jit_solution(18238877953085504274)
XLA Ops:
  0.0 0.6 iota_multiply_fusion
  0.6 0.6 iota_compare_fusion.4
  1.2 0.6 iota_compare_fusion.3
  1.8 0.6 iota_compare_fusion.2
  2.5 0.8 fusion.21
  3.3 0.7 iota_compare_fusion.5
  4.0 0.7 broadcast_multiply_fusion
  4.7 0.8 fusion.35
  5.4 0.7 fusion.34
  6.1 0.1 reshape.94
  6.2 12.6 %all-gather = bf16[4,32,3]{1,2,0:T(4,128)(2,1)S(1)} all-gather(bf16[1,32,3]{1,2,0:T(4,128)(2,1)S(1)} %fusion.35), channel_id=1, replica_groups=mesh['tm'=8,'cell'=4] {'cell'}, dimensions={0}, use_global_device_ids=true | all-gather | bytes 960 | tf_op jit(solution)/shard_map/all_gather | solution.py:53
  18.9 0.1 reshape.107
  18.9 0.7 fusion.38
  19.6 2.1 slice_bitcast_fusion
  21.7 2.2 gather_fusion
  23.9 0.9 broadcast_select_fusion
  24.8 13.6 %all_gather.6 = bf16[3,128,256]{2,1,0:T(8,128)(2,1)S(1)} all-gather(bf16[3,32,256]{2,1,0:T(8,128)(2,1)S(1)} %broadcast_select_fusion), channel_id=1, replica_groups=mesh['tm'=8,'cell'=4] {'cell'}, dimensions={1}, use_global_device_ids=true | all-gather | bytes 245760 | tf_op jit(solution)/shard_map/all_gather | solution.py:52
  38.4 0.6 fusion.15
  39.0 0.0 copy-start
  39.0 0.3 copy.52
  39.2 1.2 fusion.9
  40.4 35.2 %custom-call.17 = f32[3,128,128]{2,1,0:T(8,128)S(1)} custom-call(f32[3,128,128]{2,1,0:T(8,128)S(1)} %cholesky.122), custom_call_target="Cholesky" | custom-call | tf_op jit(solution)/shard_map/jit(cholesky)/cholesky | solution.py:33
  75.6 0.0 copy-done.3
  75.6 29.5 %custom-call.18 = f32[3,1,128,128]{2,3,1,0:T(8,128)S(1)} custom-call(f32[3,1,128,128]{3,2,1,0:T(8,128)S(1)} %select_bitcast_fusion), custom_call_target="InvertDiagBlocksLowerTriangular" | custom-call | tf_op jit(solution)/shard_map/jit(cholesky)/cholesky | solution.py:33
  105.1 0.1 cholesky.117
  105.2 0.4 constant_dynamic-update-slice_fusion.1
  105.6 0.5 convolution_subtract_fusion.1
  106.1 35.2 %custom-call.19 = f32[3,128,128]{2,1,0:T(8,128)S(1)} custom-call(f32[3,128,128]{2,1,0:T(8,128)S(1)} %convolution_subtract_fusion.1), custom_call_target="Cholesky" | custom-call | tf_op jit(solution)/shard_map/jit(cholesky)/cholesky | solution.py:33
  141.3 0.1 compare_reduce_fusion
  141.5 0.1 compare_reduce_fusion.1
  141.6 0.0 copy-done.1
  141.6 0.2 select_select_fusion
  141.8 0.1 triangular_solve.74
  141.8 5.4 %while.17 = (s32[]{:T(128)}, f32[3,256,256]{2,1,0:T(8,128)S(1)}, s32[2,2]{1,0:T(2,128)S(1)}, f32[2,3,128,128]{3,2,0,1:T(8,128)}, s32[]{:T(128)}) while((s32[]{:T(128)}, f32[3,256,256]{2,1,0:T(8,128)S(1)}, s32[2,2]{1,0:T(2,128)S(1)}, f32[2,3,128,128]{3,2,0,1:T(8,128)}, s32[]{:T(128)}) %tuple.56), condition=%wide.while_cond, body=%wide.while_body.sunk | while | flops 2 | bytes 394349 | solution.py:35
  141.8 0.6 fusion.58
  142.5 2.1 bitcast_dynamic-update-slice_fusion.2
  144.5 0.6 fusion.58
  145.1 2.1 bitcast_dynamic-update-slice_fusion.2
  147.2 59.8 %custom-call.20 = f32[3,2,128,128]{2,3,1,0:T(8,128)S(1)} custom-call(f32[3,2,128,128]{3,2,1,0:T(8,128)} %bitcast.105), custom_call_target="InvertDiagBlocksLowerTriangular" | custom-call | tf_op jit(solution)/shard_map/vmap(jit(_solve_triangular))/triangular_solve | solution.py:35
  207.0 0.0 copy-done
  207.0 0.5 fusion.25
  207.5 0.5 convolution_subtract_fusion
  208.0 0.5 fusion.24
  208.5 0.1 fusion.7
  208.7 0.6 fusion.18
  209.3 1.3 fusion.39
  210.6 1.0 stack.27
  211.6 4.2 %all-to-all-start = ((bf16[8,1,256,256]{3,2,1,0:T(8,128)(2,1)}), bf16[8,1,256,256]{3,2,1,0:T(8,128)(2,1)}, u32[]{:S(2)}, u32[]{:S(2)}) async-start(bf16[8,1,256,256]{3,2,1,0:T(8,128)(2,1)} %stack.27), calls=%async_computation | async-start | bytes 2097152 | tf_op jit(solution)/shard_map/all_to_all | solution.py:10
  215.9 15.4 %all-to-all-done = bf16[8,1,256,256]{3,2,1,0:T(8,128)(2,1)} async-done(((bf16[8,1,256,256]{3,2,1,0:T(8,128)(2,1)}), bf16[8,1,256,256]{3,2,1,0:T(8,128)(2,1)}, u32[]{:S(2)}, u32[]{:S(2)}) %all-to-all-start) | async-done | bytes 1048608 | tf_op jit(solution)/shard_map/all_to_all | solution.py:10
  231.2 1.4 bitcast_convert_fusion
  232.7 3.5 %while.16 = (s32[]{:T(128)}, f32[256,256]{1,0:T(8,128)S(1)}, s32[]{:T(128)}, f32[8,256,256]{2,1,0:T(8,128)S(1)}, s32[]{:T(128)}, /*index=5*/s32[]{:T(128)}, s32[]{:T(128)}, s32[]{:T(128)}) while((s32[]{:T(128)}, f32[256,256]{1,0:T(8,128)S(1)}, s32[]{:T(128)}, f32[8,256,256]{2,1,0:T(8,128)S(1)}, s32[]{:T(128)}, /*index=5*/s32[]{:T(128)}, ...), condition=%wide.region_5.6_spmd, body=%wide.region_4.5_spmd.sunk | while | flops 201392128 | bytes 1573017 | solution.py:74
  232.7 0.4 convolution_select_fusion.2
  233.2 0.4 convolution_select_fusion.2
  233.6 0.4 convolution_select_fusion.2
  234.0 0.4 convolution_select_fusion.2
  234.5 0.4 convolution_select_fusion.2
  234.9 0.4 convolution_select_fusion.2
  235.4 0.4 convolution_select_fusion.2
  235.8 0.4 convolution_select_fusion.2
  236.2 0.6 fusion.6
  236.8 0.4 fusion.5
  237.2 1.3 fusion.4
  238.5 7.3 %fusion.3 = bf16[3,4096,256]{1,2,0:T(8,128)(2,1)} fusion(bf16[3,4096,256]{2,1,0:T(8,128)(2,1)} %bitcast.100, bf16[1,256,256]{2,1,0:T(8,128)(2,1)S(1)} %fusion.6, bf16[1,256,256]{2,1,0:T(8,128)(2,1)S(1)} %fusion.5, bf16[1,256,256]{2,1,0:T(8,128)(2,1)S(1)} %fusion.4), kind=kOutput, calls=%fused_computation.8 | convolution fusion | flops 1614151680 | bytes 12976128 | tf_op jit(solution)/shard_map/wcm,wmn->wcn/dot_general | solution.py:80
  245.8 8.6 %copy.65 = bf16[3,4096,256]{2,1,0:T(8,128)(2,1)} copy(bf16[3,4096,256]{1,2,0:T(8,128)(2,1)} %fusion.3) | data formatting | bytes 12582912 | tf_op jit(solution)/shard_map/reshape | solution.py:81
  (23 shorter events, 0.3 us)
Async XLA Ops:
  23.8 51.8 %copy-start.3 = (pred[128,128]{1,0:T(8,128)(4,1)S(1)}, pred[128,128]{1,0:T(8,128)(4,1)}, u32[]{:S(2)}) copy-start(pred[128,128]{1,0:T(8,128)(4,1)} %iota_compare_fusion.3) | copy-start | bytes 49156
  23.9 117.4 %copy-start.2 = (pred[128,128]{1,0:T(8,128)(4,1)S(1)}, pred[128,128]{1,0:T(8,128)(4,1)}, u32[]{:S(2)}) copy-start(pred[128,128]{1,0:T(8,128)(4,1)} %iota_compare_fusion.4) | copy-start | bytes 49156
  23.9 117.7 %copy-start.1 = (pred[256,256]{1,0:T(8,128)(4,1)S(1)}, pred[256,256]{1,0:T(8,128)(4,1)}, u32[]{:S(2)}) copy-start(pred[256,256]{1,0:T(8,128)(4,1)} %iota_compare_fusion.2) | copy-start | bytes 196612
  23.9 117.9 %copy-start.4 = (s32[2]{0:T(128)S(1)}, s32[2]{0:T(128)}, u32[]{:S(2)}) copy-start(s32[2]{0:T(128)} %iota_multiply_fusion) | copy-start | bytes 28
  39.0 168.0 %copy-start = (f32[128,256]{1,0:T(8,128)S(1)}, f32[128,256]{1,0:T(8,128)}, u32[]{:S(2)}) copy-start(f32[128,256]{1,0:T(8,128)} %get-tuple-element.145) | copy-start | bytes 393220
  211.6 19.6 %all-to-all-start = ((bf16[8,1,256,256]{3,2,1,0:T(8,128)(2,1)}), bf16[8,1,256,256]{3,2,1,0:T(8,128)(2,1)}, u32[]{:S(2)}, u32[]{:S(2)}) async-start(bf16[8,1,256,256]{3,2,1,0:T(8,128)(2,1)} %stack.27), calls=%async_computation | async-start | bytes 2097152 | tf_op jit(solution)/shard_map/all_to_all | solution.py:10
